TPU v7x, 32 devices: a 4x4x1 block of a 4x4x8 slice. The times are simulated.
32 devices in a mesh: dp: 1 (over z), tp: 4 (over y), cp: 8 (over x, core).
Axes of the slice: x: 4, y: 4, z: 1, core: 2. Of those that a mesh axis runs over, the one named last changes fastest.
The devices are a block of a 4x4x8 slice.
Arguments:
- hidden: bfloat16 [16, 64, 5120], P('dp')
- attn_gain: bfloat16 [5120], replicated
- w_query: bfloat16 [5120, 4096], P(None, 'tp')
- w_key: bfloat16 [5120, 1024], P(None, 'tp')
- w_value: bfloat16 [5120, 1024], P(None, 'tp')
- w_out: bfloat16 [4096, 5120], P('tp')
- cache_k: bfloat16 [16, 4, 8, 8, 256, 128], P('dp', None, 'cp', 'tp')
- cache_v: bfloat16 [16, 4, 8, 8, 256, 128], P('dp', None, 'cp', 'tp')
- ctx_len: int32 [16], P('dp')
- positions: int32 [16, 64], P('dp')
- tree_mask: int32 [16, 64, 64], P('dp')
Outputs:
- output 1: bfloat16 [16, 64, 5120], P('dp')
- output 2: bfloat16 [16, 4, 8, 8, 256, 128], P('dp', None, 'cp', 'tp')
- output 3: bfloat16 [16, 4, 8, 8, 256, 128], P('dp', None, 'cp', 'tp')
All inputs are finite; a program needn't handle non-finite values.
Results may differ from a plain program's by a relative error of at most 0.0082716.
Values sent between devices are 32-bit elements.
A program may use at most 768 MiB of HBM per device.

v0:
```python
import math
import jax
import jax.numpy as jnp
from jax import lax
from jax.sharding import PartitionSpec as P

ROPE_THETA = 500000.0
NORM_EPS = 1e-5
MASKED = -1e30


def rope_tables(positions, head_dim):
    freq_idx = jnp.arange(head_dim // 2, dtype=jnp.float32)
    inv_freq = 1.0 / (ROPE_THETA ** (2.0 * freq_idx / head_dim))
    wavelen = 2.0 * math.pi / inv_freq
    smooth = (8192.0 / wavelen - 1.0) / 3.0
    blended = (1.0 - smooth) * inv_freq / 8.0 + smooth * inv_freq
    inv_freq = jnp.where(wavelen < 2048.0, inv_freq, jnp.where(wavelen > 8192.0, inv_freq / 8.0, blended))
    angle = positions.astype(jnp.float32)[..., None] * inv_freq
    return jnp.cos(angle)[..., None, :], jnp.sin(angle)[..., None, :]


def apply_rope(values, cos_tab, sin_tab):
    half = values.shape[-1] // 2
    first = values[..., :half]
    second = values[..., half:]
    return jnp.concatenate([first * cos_tab - second * sin_tab, second * cos_tab + first * sin_tab], axis=-1)


def rms_norm(hidden, attn_gain):
    wide = hidden.astype(jnp.float32)
    inv_rms = lax.rsqrt(jnp.mean(wide * wide, axis=-1, keepdims=True) + NORM_EPS)
    return wide, (wide * inv_rms * attn_gain.astype(jnp.float32)).astype(jnp.bfloat16)


def solution(mesh):
    cp_size = mesh.shape['cp']
    cache_spec = P('dp', None, 'cp', 'tp')
    row_spec = P('dp')

    def local_step(hidden, attn_gain, w_query, w_key, w_value, w_out, cache_k, cache_v, ctx_len, positions, tree_mask):
        num_reqs, tree_len, width = hidden.shape
        num_blocks = cache_k.shape[1]
        kv_local = cache_k.shape[3]
        blk_len = cache_k.shape[4]
        head_dim = cache_k.shape[5]
        heads_local = w_query.shape[1] // head_dim
        group = heads_local // kv_local
        cp_rank = lax.axis_index('cp')
        scale = head_dim ** -0.5
        wide, normed = rms_norm(hidden, attn_gain)
        flat_rows = normed.reshape(num_reqs * tree_len, width)
        query = jnp.dot(flat_rows, w_query, preferred_element_type=jnp.float32).reshape(num_reqs, tree_len, heads_local, head_dim)
        key_new = jnp.dot(flat_rows, w_key, preferred_element_type=jnp.float32).reshape(num_reqs, tree_len, kv_local, head_dim)
        val_new = jnp.dot(flat_rows, w_value, preferred_element_type=jnp.float32).astype(jnp.bfloat16).reshape(num_reqs, tree_len, kv_local, head_dim)
        cos_tab, sin_tab = rope_tables(positions, head_dim)
        query = apply_rope(query, cos_tab, sin_tab).astype(jnp.bfloat16).reshape(num_reqs, tree_len, kv_local, group, head_dim)
        key_new = apply_rope(key_new, cos_tab, sin_tab).astype(jnp.bfloat16)
        keys = cache_k[:, :, 0]
        values = cache_v[:, :, 0]
        score_cache = jnp.einsum('rtkgd,rjkid->rtkgji', query, keys, preferred_element_type=jnp.float32) * scale
        block_pos = (jnp.arange(num_blocks)[:, None] * cp_size + cp_rank) * blk_len + jnp.arange(blk_len)[None, :]
        valid = (block_pos[None] < ctx_len[:, None, None])[:, None, None, None]
        score_tree = jnp.einsum('rtkgd,rskd->rtkgs', query, key_new, preferred_element_type=jnp.float32) * scale
        tree_ok = ((tree_mask > 0) & (cp_rank == 0))[:, :, None, None, :]
        score_cache = jnp.where(valid, score_cache, MASKED)
        score_tree = jnp.where(tree_ok, score_tree, MASKED)
        row_max = jnp.maximum(score_cache.max(axis=(4, 5)), score_tree.max(axis=-1))
        prob_cache = jnp.where(valid, jnp.exp(score_cache - row_max[..., None, None]), 0.0)
        prob_tree = jnp.where(tree_ok, jnp.exp(score_tree - row_max[..., None]), 0.0)
        row_sum = prob_cache.sum(axis=(4, 5)) + prob_tree.sum(axis=-1)
        out_part = jnp.einsum('rtkgji,rjkid->rtkgd', prob_cache.astype(jnp.bfloat16), values, preferred_element_type=jnp.float32)
        out_part = out_part + jnp.einsum('rtkgs,rskd->rtkgd', prob_tree.astype(jnp.bfloat16), val_new, preferred_element_type=jnp.float32)
        glob_max = lax.pmax(row_max, 'cp')
        factor = jnp.exp(row_max - glob_max)
        glob_sum = lax.psum(row_sum * factor, 'cp')
        glob_out = lax.psum(out_part * factor[..., None], 'cp')
        attn_out = (glob_out / glob_sum[..., None]).astype(jnp.bfloat16).reshape(num_reqs, tree_len, heads_local * head_dim)
        proj_part = jnp.einsum('rtf,fe->rte', attn_out, w_out, preferred_element_type=jnp.float32).astype(jnp.bfloat16)
        proj_sum = lax.psum(proj_part.astype(jnp.float32), 'tp')
        out_hidden = (wide + proj_sum).astype(jnp.bfloat16)
        slot_ids = ctx_len[:, None] + jnp.arange(tree_len)[None, :]
        block_ids = slot_ids // blk_len
        local_blk = jnp.where(block_ids % cp_size == cp_rank, block_ids // cp_size, num_blocks)
        req_ids = jnp.broadcast_to(jnp.arange(num_reqs)[:, None], (num_reqs, tree_len))
        new_keys = keys.at[req_ids, local_blk, :, slot_ids % blk_len, :].set(key_new, mode='drop')
        new_vals = values.at[req_ids, local_blk, :, slot_ids % blk_len, :].set(val_new, mode='drop')
        return out_hidden, new_keys[:, :, None], new_vals[:, :, None]

    program = jax.shard_map(local_step, mesh=mesh, in_specs=(row_spec, P(), P(None, 'tp'), P(None, 'tp'), P(None, 'tp'), P('tp', None), cache_spec, cache_spec, row_spec, row_spec, row_spec), out_specs=(row_spec, cache_spec, cache_spec), check_vma=False)
    return program
```

profile of v0, /device:TPU:97, one launch (start us, length us, event | category | flops | bytes accessed | tf_op | source)
XLA Modules:
  0.0 646.5 jit_solution(8426227481337932856)
XLA Ops:
  7.2 0.0 copy-start
  7.2 0.1 all-reduce.3.cloned.1.call-start
  7.3 0.1 iota_add_fusion.1
  7.4 13.8 %copy.86 = bf16[1024,5120]{1,0:T(8,128)(2,1)} copy(bf16[1024,5120]{0,1:T(8,128)(2,1)} %bitcast.125) | data formatting | bytes 20971520 | tf_op jit(solution)/shard_map/dot_general | solution.py:53
  21.2 0.0 copy-done.6
  21.2 6.1 fusion.4
  27.4 0.0 copy-done.7
  27.4 0.0 copy-done.5
  27.4 0.1 compare_and_fusion
  27.5 0.3 copy.61
  27.8 4.4 copy.90
  32.2 6.5 %fusion.6 = bf16[16,64,5120]{2,1,0:T(8,128)(2,1)S(1)} fusion(bf16[16,64,5120]{2,1,0:T(8,128)(2,1)} %param.11, f32[5120]{0:T(1024)S(1)} %convert_element_type.37, f32[16,64]{1,0:T(8,128)S(1)} %add_rsqrt_fusion), kind=kLoop, calls=%fused_computation.14 | loop fusion | flops 20971520 | bytes 20996096 | tf_op jit(solution)/shard_map/convert_element_type | solution.py:33
  38.7 0.0 copy-start.2
  38.7 0.0 copy-start.3
  38.7 18.1 %fusion.16 = f32[16,64,8,128]{3,1,2,0:T(8,128)S(1)} fusion(bf16[8,128,5120,1]{2,1,0,3:T(8,128)(2,1)} %bitcast.127, bf16[16,64,5120]{2,1,0:T(8,128)(2,1)S(1)} %fusion.6), kind=kOutput, calls=%fused_computation.23 | convolution fusion | flops 10737418240 | bytes 25165824 | tf_op jit(solution)/shard_map/dot_general | solution.py:53
  56.8 0.0 copy-done.2
  56.8 0.0 copy-done.3
  56.8 2.9 fusion.14
  59.7 1.9 multiply_cosine_fusion
  61.6 0.0 copy-start.8
  61.6 3.8 subtract_convert_fusion
  65.4 0.5 subtract_convert_fusion.1
  65.9 0.0 copy-done.8
  65.9 0.1 broadcast_compare_fusion
  66.0 0.3 pad_maximum_fusion.1
  66.3 16.5 %bitcast_reduce_fusion = (f32[16,64,2,4]{1,3,2,0:T(4,128)S(1)}, f32[16,2,64,4,4,256]{5,2,4,3,1,0:T(8,128)}) fusion(pred[16,4,256]{2,1,0:T(4,128)(4,1)S(1)} %broadcast_compare_fusion, bf16[16,64,2,4,64]{4,1,3,2,0:T(8,128)(2,1)} %bitcast.123, bf16[16,64,2,4,64]{4,1,3,2,0:T(8,128)(2,1)} %bitcast.121, bf16[16,4,1,2,256,128]{5,4,3,2,1,0:T(8,128)(2,1)} %param.17), kind=kOutput, calls=%fused_computation.3 | convolution fusion | flops 2176835584 | bytes 44089344 | tf_op jit(solution)/shard_map/rtkgd,rjkid->rtkgji/dot_general | solution.py:61
  82.8 6.6 %fusion.24 = (f32[16,64,2,4]{1,3,2,0:T(4,128)S(1)}, f32[16,2,64,64,4]{3,2,4,1,0:T(8,128)}) fusion(pred[16,64,64]{1,2,0:T(8,128)(4,1)S(1)} %copy.61, bf16[16,64,2,4,64]{4,1,3,2,0:T(8,128)(2,1)} %bitcast.124, bf16[16,64,2,4,64]{4,1,3,2,0:T(8,128)(2,1)} %bitcast.122, bf16[16,64,2,128]{3,1,2,0:T(8,128)(2,1)S(1)} %pad_maximum_fusion.1), kind=kOutput, calls=%fused_computation.36 | convolution fusion | flops 139976704 | bytes 4816896 | tf_op jit(solution)/shard_map/rtkgd,rskd->rtkgs/dot_general | solution.py:64
  89.4 24.7 %pmax.7 = f32[16,64,2,4]{1,3,2,0:T(4,128)S(1)} all-reduce(f32[16,64,2,4]{1,3,2,0:T(4,128)S(1)} %max.13), channel_id=1, replica_groups=mesh['dp'=1,'tp'=4,'cp'=8] {'cp'}, use_global_device_ids=true, to_apply=%region_3.4 | all-reduce | flops 8192 | bytes 65536 | tf_op jit(solution)/shard_map/pmax | solution.py:74
  114.1 15.3 %fusion.2 = f32[16,64,2,4]{1,3,2,0:T(4,128)S(1)} fusion(f32[16,2,64,4,4,256]{5,2,4,3,1,0:T(8,128)} %get-tuple-element.23, f32[16,64,2,4]{1,3,2,0:T(4,128)S(1)} %max.13, pred[16,4,256]{2,1,0:T(4,128)(4,1)S(1)} %broadcast_compare_fusion), kind=kLoop, calls=%fused_computation.10 | loop fusion | flops 41934848 | bytes 33636352 | tf_op jit(solution)/shard_map/reduce_sum | solution.py:71
  129.4 19.3 %fusion.8 = f32[16,2,64,4,128,1]{4,2,5,3,1,0:T(8,128)} fusion(f32[16,2,64,4,4,256]{5,2,4,3,1,0:T(8,128)} %get-tuple-element.23, f32[16,64,2,4]{1,3,2,0:T(4,128)S(1)} %max.13, pred[16,4,256]{2,1,0:T(4,128)(4,1)S(1)} %broadcast_compare_fusion, bf16[16,4,1,2,256,128]{5,4,3,2,1,0:T(8,128)(2,1)} %param.18), kind=kOutput, calls=%fused_computation.16 | convolution fusion | flops 2189426688 | bytes 46186496 | tf_op jit(solution)/shard_map/rtkgji,rjkid->rtkgd/dot_general | solution.py:72
  148.7 3.6 fusion.25
  152.3 0.0 copy-done
  152.3 7.7 %convolution_convert_fusion = bf16[1024,256]{0,1:T(8,128)(2,1)} fusion(bf16[1024,5120]{1,0:T(8,128)(2,1)} %bitcast.126, bf16[5120,256]{1,0:T(8,128)(2,1)S(1)} %copy-done), kind=kOutput, calls=%fused_computation.46 | convolution fusion | flops 2684616704 | bytes 13631488 | tf_op jit(solution)/shard_map/dot_general | solution.py:55
  160.0 1.8 reshape.358
  161.8 6.1 fusion.23
  167.9 0.1 all-reduce.3.cloned.1.call-update
  167.9 0.1 all-reduce.5.cloned.1.call-start
  168.0 25.8 %psum.22 = f32[16,64,2,4]{1,3,2,0:T(4,128)S(1)} all-reduce(f32[16,64,2,4]{1,3,2,0:T(4,128)S(1)} %bitcast.137), channel_id=1, replica_groups=mesh['dp'=1,'tp'=4,'cp'=8] {'cp'}, use_global_device_ids=true, to_apply=%region_7.8 | all-reduce | flops 8192 | bytes 65536 | tf_op jit(solution)/shard_map/psum | solution.py:76
  193.7 43.1 %all-reduce.3.cloned.1.call-done = f32[16,64,2,4,128]{4,1,3,2,0:T(8,128)} async-done(((f32[16,64,2,4,128]{4,1,3,2,0:T(8,128)}), f32[16,64,2,4,128]{4,1,3,2,0:T(8,128)}) %all-reduce.3.cloned.1.call-update) | async-done | bytes 4194320 | tf_op jit(solution)/shard_map/psum | solution.py:77
  236.9 2.9 divide_convert_fusion
  239.8 3.0 copy.68
  242.8 3.2 reshape.326
  246.0 17.6 %convert_convert_fusion = f32[16,64,5120]{2,1,0:T(8,128)} fusion(bf16[16,64,1024]{2,1,0:T(8,128)(2,1)S(1)} %reshape.326, bf16[1024,5120]{1,0:T(8,128)(2,1)} %param.16), kind=kOutput, calls=%fused_computation.25 | convolution fusion | flops 10747904000 | bytes 33554432 | tf_op jit(solution)/shard_map/rtf,fe->rte/dot_general | solution.py:79
  263.7 0.1 all-reduce.5.cloned.1.call-update
  263.7 7.9 %copy.59 = bf16[16,4,1,2,256,128]{5,4,1,0,3,2:T(8,128)(2,1)} copy(bf16[16,4,1,2,256,128]{5,4,3,2,1,0:T(8,128)(2,1)} %param.17) | data formatting | bytes 16777216 | tf_op args[6]
  271.7 7.9 %copy.63 = bf16[16,4,1,2,256,128]{5,4,1,0,3,2:T(8,128)(2,1)} copy(bf16[16,4,1,2,256,128]{5,4,3,2,1,0:T(8,128)(2,1)} %param.18) | data formatting | bytes 16777216 | tf_op args[7]
  279.6 16.4 %copy.70 = bf16[16384,2,128]{2,1,0:T(2,128)(2,1)} copy(bf16[16384,2,128]{2,0,1:T(8,128)(2,1)} %bitcast.118) | data formatting | bytes 16777216
  296.0 0.0 copy-done.9
  296.0 0.1 compare_select_fusion.1
  296.1 0.0 copy-done.10
  296.1 0.1 multiply_reduce_fusion
  296.2 0.1 and_reduce_fusion
  296.3 0.1 reshape.335
  296.3 0.5 copy.71
  296.9 90.2 %scatter_fusion = bf16[16384,2,128]{2,1,0:T(2,128)(2,1)} fusion(bf16[16384,2,128]{2,1,0:T(2,128)(2,1)} %copy.70, s32[1024]{0:T(1024)S(1)} %reshape.335, bf16[1024,2,128]{2,1,0:T(2,128)(2,1)S(1)} %copy.71), kind=kCustom, calls=%fused_computation | custom fusion | bytes 1576960
  387.1 7.8 %copy.72 = bf16[16384,2,128]{2,0,1:T(8,128)(2,1)} copy(bf16[16384,2,128]{2,1,0:T(2,128)(2,1)} %scatter_fusion) | data formatting | bytes 16777216
  394.9 7.9 %copy.76 = bf16[16,4,1,2,256,128]{5,4,3,2,1,0:T(8,128)(2,1)} copy(bf16[16,4,1,2,256,128]{5,4,1,0,3,2:T(8,128)(2,1)} %bitcast.119) | data formatting | bytes 16777216
  402.8 16.4 %copy.73 = bf16[16384,2,128]{2,1,0:T(2,128)(2,1)} copy(bf16[16384,2,128]{2,0,1:T(8,128)(2,1)} %bitcast.117) | data formatting | bytes 16777216
  419.3 0.7 copy.74
  419.9 90.2 %scatter_fusion.1 = bf16[16384,2,128]{2,1,0:T(2,128)(2,1)} fusion(bf16[16384,2,128]{2,1,0:T(2,128)(2,1)} %copy.73, s32[1024]{0:T(1024)S(1)} %reshape.335, bf16[1024,2,128]{2,1,0:T(2,128)(2,1)S(1)} %copy.74), kind=kCustom, calls=%fused_computation.1 | custom fusion | bytes 1576960
  510.2 7.8 %copy.75 = bf16[16384,2,128]{2,0,1:T(8,128)(2,1)} copy(bf16[16384,2,128]{2,1,0:T(2,128)(2,1)} %scatter_fusion.1) | data formatting | bytes 16777216
  518.0 7.9 %copy.77 = bf16[16,4,1,2,256,128]{5,4,3,2,1,0:T(8,128)(2,1)} copy(bf16[16,4,1,2,256,128]{5,4,1,0,3,2:T(8,128)(2,1)} %bitcast.120) | data formatting | bytes 16777216
  525.9 97.5 %all-reduce.5.cloned.1.call-done = f32[16,64,5120]{2,1,0:T(8,128)} async-done(((f32[16,64,5120]{2,1,0:T(8,128)}), f32[16,64,5120]{2,1,0:T(8,128)}) %all-reduce.5.cloned.1.call-update) | async-done | bytes 20971536 | tf_op jit(solution)/shard_map/psum | solution.py:80
  623.4 15.8 %fusion.7 = bf16[16,64,5120]{2,1,0:T(8,128)(2,1)} fusion(f32[16,64,5120]{2,1,0:T(8,128)} %all-reduce.5.cloned.1.call-done, bf16[16,64,5120]{2,1,0:T(8,128)(2,1)} %param.11), kind=kLoop, calls=%fused_computation.15 | loop fusion | flops 15728640 | bytes 41943040 | tf_op jit(solution)/shard_map/convert_element_type | solution.py:81
  (21 shorter events, 0.2 us)
Async XLA Ops:
  7.2 145.1 %copy-start = (bf16[5120,256]{1,0:T(8,128)(2,1)S(1)}, bf16[5120,256]{1,0:T(8,128)(2,1)}, u32[]{:S(2)}) copy-start(bf16[5120,256]{1,0:T(8,128)(2,1)} %param.15) | copy-start | bytes 7864324
  7.2 229.7 %all-reduce.3.cloned.1.call-start = ((), (), s32[]{:S(2)}) async-start(), calls=%async_computation | async-start | bytes 8388608 | tf_op jit(solution)/shard_map/psum | solution.py:77
  7.4 13.8 %copy-start.6 = (bf16[5120]{0:T(1024)(128)(2,1)S(1)}, bf16[5120]{0:T(1024)(128)(2,1)}, u32[]{:S(2)}) copy-start(bf16[5120]{0:T(1024)(128)(2,1)} %param.12) | copy-start | bytes 30724
  21.2 6.2 copy-start.7
  21.2 6.2 copy-start.5
  38.7 18.1 %copy-start.2 = (bf16[16,64,5120]{2,1,0:T(8,128)(2,1)}, bf16[16,64,5120]{2,1,0:T(8,128)(2,1)S(1)}, u32[]{:S(2)}) copy-start(bf16[16,64,5120]{2,1,0:T(8,128)(2,1)S(1)} %fusion.6) | copy-start | bytes 31457284
  38.7 18.1 %copy-start.3 = (bf16[256,5120]{1,0:T(8,128)(2,1)S(1)}, bf16[256,5120]{1,0:T(8,128)(2,1)}, u32[]{:S(2)}) copy-start(bf16[256,5120]{1,0:T(8,128)(2,1)} %copy.90) | copy-start | bytes 7864324
  61.6 4.3 copy-start.8
  167.9 455.5 %all-reduce.5.cloned.1.call-start = ((), (), s32[]{:S(2)}) async-start(), calls=%async_computation.1 | async-start | bytes 41943040 | tf_op jit(solution)/shard_map/psum | solution.py:80
  279.5 16.4 %copy-start.9 = (s32[16]{0:T(128)S(1)}, s32[16]{0:T(128)}, u32[]{:S(2)}) copy-start(s32[16]{0:T(128)} %param.19) | copy-start | bytes 196
  279.5 16.5 %copy-start.10 = (s32[3]{0:T(128)S(1)}, s32[3]{0:T(128)}, u32[]{:S(2)}) copy-start(s32[3]{0:T(128)} %constant.107) | copy-start | bytes 40
  279.5 16.6 %copy-start.11 = (s32[3]{0:T(128)S(1)}, s32[3]{0:T(128)}, u32[]{:S(2)}) copy-start(s32[3]{0:T(128)} %constant.110) | copy-start | bytes 40
  402.8 16.4 %copy-start.4 = (bf16[1024,256]{0,1:T(8,128)(2,1)S(1)}, bf16[1024,256]{0,1:T(8,128)(2,1)}, u32[]{:S(2)}) copy-start(bf16[1024,256]{0,1:T(8,128)(2,1)} %convolution_convert_fusion) | copy-start | bytes 1572868
  623.4 15.8 %copy-start.1 = (bf16[5120,256]{1,0:T(8,128)(2,1)S(1)}, bf16[5120,256]{1,0:T(8,128)(2,1)}, u32[]{:S(2)}) copy-start(bf16[5120,256]{1,0:T(8,128)(2,1)} %param.15) | copy-start | bytes 7864324
Sparse Core Ops, SparseCore 0:
  168.0 68.8 all-reduce.2
  263.8 359.5 all-reduce.4
where the time goes:
time: 656 us; the launch traced here: 647 us
  local copies, waits for them, and re-layouts  288 us (44%)
  waiting for transfers between devices  141 us (21%)
  matrix products  94.6 us (14%)
  other arithmetic  57.3 us (9%)
  blocking collectives  50.4 us (8%)
  between operations  14.8 us (2%)
    unnamed x35, local copies, waits for them, and re-layouts  261 us
    psum x1, waiting for transfers between devices, local_step(): proj_sum = lax.psum(proj_part.astype(jnp.float32), 'tp')  97.5 us
    psum x1, waiting for transfers between devices, local_step(): glob_out = lax.psum(out_part * factor[..., None], 'cp')  43.1 us
    psum x1, blocking collectives, local_step(): glob_sum = lax.psum(row_sum * factor, 'cp')  25.8 us
    pmax x1, blocking collectives, local_step(): glob_max = lax.pmax(row_max, 'cp')  24.7 us
    dot_general x1, matrix products, local_step(): jnp.einsum('rtkgji,rjkid->rtkgd', prob_cache.astype(jnp.bfloat16), values...  19.3 us
    reduce_sum x2, other arithmetic, local_step(): row_sum = prob_cache.sum(axis=(4, 5)) + prob_tree.sum(axis=-1)  19 us
    dot_general x1, matrix products, local_step(): jnp.dot(flat_rows, w_query, preferred_element_type=jnp.float32)  18.1 us
  transfers between devices with their start and end apart: 2, of which 2 were waited for; matrix products, arithmetic and copies ran while one was open for 41% of the time, Pallas kernels for 0%

commit v1 on v0

v1 whole, which is shorter than its diff:
```python
import functools
import math

import jax
import jax.numpy as jnp
from jax import lax
from jax.experimental import pallas as pl
from jax.experimental.pallas import tpu as pltpu
from jax.sharding import PartitionSpec as P

MESH = pl.DeviceIdType.MESH
ROPE_THETA = 500000.0
NORM_EPS = 1e-5
MASKED = -1e30
NUM_CHUNKS = 2
STAT_ROWS = 8
F32 = jnp.float32
BF16 = jnp.bfloat16


def rope_tables(positions, head_dim):
    freq_idx = jnp.arange(head_dim // 2, dtype=F32)
    inv_freq = 1.0 / (ROPE_THETA ** (2.0 * freq_idx / head_dim))
    wavelen = 2.0 * math.pi / inv_freq
    smooth = (8192.0 / wavelen - 1.0) / 3.0
    blended = (1.0 - smooth) * inv_freq / 8.0 + smooth * inv_freq
    inv_freq = jnp.where(wavelen < 2048.0, inv_freq, jnp.where(wavelen > 8192.0, inv_freq / 8.0, blended))
    angle = positions.astype(F32).reshape(-1)[:, None] * inv_freq
    cos_tab, sin_tab = jnp.cos(angle), jnp.sin(angle)
    return jnp.concatenate([cos_tab, cos_tab], axis=-1), jnp.concatenate([-sin_tab, sin_tab], axis=-1)


def qkv_kernel(x_ref, gain_ref, cos_ref, sin_ref, wq_ref, wk_ref, wv_ref, q_ref, k_ref, v_ref):
    head_dim = cos_ref.shape[1]
    wide = x_ref[...].astype(F32)
    inv_rms = lax.rsqrt(jnp.mean(wide * wide, axis=-1, keepdims=True) + NORM_EPS)
    normed = (wide * inv_rms * gain_ref[...].astype(F32)).astype(BF16)
    cos_tab, sin_tab = cos_ref[...], sin_ref[...]

    def rotate(full, out_ref):
        for h in range(full.shape[1] // head_dim):
            part = full[:, h * head_dim:(h + 1) * head_dim]
            out_ref[:, h * head_dim:(h + 1) * head_dim] = (part * cos_tab + pltpu.roll(part, head_dim // 2, 1) * sin_tab).astype(BF16)

    rotate(jnp.dot(normed, wq_ref[...], preferred_element_type=F32), q_ref)
    rotate(jnp.dot(normed, wk_ref[...], preferred_element_type=F32), k_ref)
    v_ref[...] = jnp.dot(normed, wv_ref[...], preferred_element_type=F32).astype(BF16)


def project_qkv(x_rows, gain, cos_tab, sin_tab, wq, wk, wv):
    rows, width = x_rows.shape
    tile = min(128, rows)
    row_block = lambda n: pl.BlockSpec((tile, n), lambda i: (i, 0))
    whole = lambda a: pl.BlockSpec(a.shape, lambda i: (0, 0), pipeline_mode=pl.Buffered(1))
    return pl.pallas_call(
        qkv_kernel,
        grid=(rows // tile,),
        in_specs=[row_block(width), whole(gain), row_block(cos_tab.shape[1]), row_block(cos_tab.shape[1]), whole(wq), whole(wk), whole(wv)],
        out_specs=[row_block(wq.shape[1]), row_block(wk.shape[1]), row_block(wv.shape[1])],
        out_shape=[jax.ShapeDtypeStruct((rows, w.shape[1]), BF16) for w in (wq, wk, wv)],
        compiler_params=pltpu.CompilerParams(dimension_semantics=("arbitrary",)),
        name="qkv",
    )(x_rows, gain, cos_tab, sin_tab, wq, wk, wv)


def attn_kernel(cp_size, halves, ctx_ref, cp_ref, q_ref, kn_ref, vn_ref, mask_ref, kc_ref, vc_ref, a_ref, nk_ref, nv_ref):
    num_blocks, kv_local, blk_len, head_dim = kc_ref.shape
    tree_len = q_ref.shape[0]
    group = q_ref.shape[1] // (kv_local * head_dim)
    sub = tree_len // halves
    lanes = group * tree_len
    ctx = ctx_ref[pl.program_id(0)]
    cp_rank = cp_ref[0]
    scale = head_dim ** -0.5 * math.log2(math.e)
    nk_ref[...] = kc_ref[...]
    nv_ref[...] = vc_ref[...]
    mask = mask_ref[...].astype(F32)
    mask_rows = jnp.concatenate([mask[hf * sub:(hf + 1) * sub] for hf in range(halves) for _ in range(group)], axis=0)
    tree_ok = (mask_rows.T > 0) & (cp_rank == 0)
    for kv in range(kv_local):
        q_rows = jnp.concatenate(
            [q_ref[hf * sub:(hf + 1) * sub, (kv * group + g) * head_dim:(kv * group + g + 1) * head_dim] for hf in range(halves) for g in range(group)], axis=0)
        kn = kn_ref[:, kv * head_dim:(kv + 1) * head_dim]
        vn = vn_ref[:, kv * head_dim:(kv + 1) * head_dim]
        nt = (((1,), (1,)), ((), ()))
        tn = (((0,), (0,)), ((), ()))
        scores = []
        for j in range(num_blocks):
            s = lax.dot_general(kc_ref[j, kv], q_rows, nt, preferred_element_type=F32)
            if j >= num_blocks // 2:
                pos = (j * cp_size + cp_rank) * blk_len + lax.broadcasted_iota(jnp.int32, s.shape, 0)
                s = jnp.where(pos < ctx, s, MASKED)
            scores.append(s)
        s = lax.dot_general(kn, q_rows, nt, preferred_element_type=F32)
        scores.append(jnp.where(tree_ok, s, MASKED))
        row_max = functools.reduce(jnp.maximum, [s.max(axis=0, keepdims=True) for s in scores])
        row_sum, out = 0.0, 0.0
        for j, s in enumerate(scores):
            p = jnp.exp2((s - row_max) * scale)
            row_sum = row_sum + p.sum(axis=0, keepdims=True)
            vals = vc_ref[j, kv] if j < num_blocks else vn
            out = out + lax.dot_general(vals, p.astype(BF16), tn, preferred_element_type=F32)
        stat = jnp.where(lax.broadcasted_iota(jnp.int32, (STAT_ROWS, lanes), 0) < STAT_ROWS // 2, row_max, row_sum)
        width = lanes // halves
        for hf in range(halves):
            a_ref[hf, kv, :head_dim] = out[:, hf * width:(hf + 1) * width]
            a_ref[hf, kv, head_dim:] = stat[:, hf * width:(hf + 1) * width]
    first = ctx // blk_len
    for extra in range(2):
        blk = first + extra
        loc = blk // cp_size

        @pl.when((blk % cp_size == cp_rank) & (loc < num_blocks))
        def _():
            source = lax.broadcasted_iota(jnp.int32, (blk_len, tree_len), 0) + (blk * blk_len - ctx)
            pick = (source == lax.broadcasted_iota(jnp.int32, (blk_len, tree_len), 1)).astype(BF16)
            at = lax.broadcasted_iota(jnp.int32, (blk_len, head_dim), 0) + (blk * blk_len - ctx)
            inside = (at >= 0) & (at < tree_len)
            for kv in range(kv_local):
                for new_ref, old_ref, out_ref in ((kn_ref, kc_ref, nk_ref), (vn_ref, vc_ref, nv_ref)):
                    moved = jnp.dot(pick, new_ref[:, kv * head_dim:(kv + 1) * head_dim], preferred_element_type=F32)
                    out_ref[loc, kv] = jnp.where(inside, moved, old_ref[loc, kv].astype(F32)).astype(BF16)


def attend(cp_size, halves, ctx_len, cp_rank, q, kn, vn, tree_mask, cache_k, cache_v):
    num_reqs, num_blocks, _, kv_local, blk_len, head_dim = cache_k.shape
    tree_len = tree_mask.shape[1]
    group = q.shape[1] // (kv_local * head_dim)
    lanes = group * tree_len // halves
    rows = lambda a: pl.BlockSpec((tree_len, a.shape[1]), lambda i, *_: (i, 0))
    cache = pl.BlockSpec((None, num_blocks, None, kv_local, blk_len, head_dim), lambda i, *_: (i, 0, 0, 0, 0, 0))
    a_shape = (num_reqs, halves, kv_local, head_dim + STAT_ROWS, lanes)
    return pl.pallas_call(
        functools.partial(attn_kernel, cp_size, halves),
        grid_spec=pltpu.PrefetchScalarGridSpec(
            num_scalar_prefetch=2, grid=(num_reqs,),
            in_specs=[rows(q), rows(kn), rows(vn), pl.BlockSpec((None, tree_len, tree_len), lambda i, *_: (i, 0, 0)), cache, cache],
            out_specs=[pl.BlockSpec((None,) + a_shape[1:], lambda i, *_: (i, 0, 0, 0, 0)), cache, cache]),
        out_shape=[jax.ShapeDtypeStruct(a_shape, F32), jax.ShapeDtypeStruct(cache_k.shape, BF16), jax.ShapeDtypeStruct(cache_v.shape, BF16)],
        compiler_params=pltpu.CompilerParams(dimension_semantics=("arbitrary",)),
        name="attn",
    )(ctx_len, cp_rank, q, kn, vn, tree_mask, cache_k, cache_v)


def combine_kernel(num_chunks, nx, ny, scale, a_ref, hid_ref, w_hbm, y_hbm, w_ref, xres, d2d, step1, step2, heads_ref, part, tp1, tp2, full, stage,
                   w_sem, x_sem, out_sem, rs_send, rs_recv, ag_send, ag_recv, pr_send, pr_recv):
    head_dim = a_ref.shape[4] - STAT_ROWS
    kv_local = a_ref.shape[3]
    lanes = a_ref.shape[5]
    toks = heads_ref.shape[0]
    rows = xres.shape[1]
    width = xres.shape[2]
    group = lanes // toks
    quarter = width // 4
    half = width // 2
    cp = lax.axis_index('cp')
    me_x, core = cp // 2, cp % 2
    me_y = lax.axis_index('tp')
    other = 1 - core
    xs = [me_x] + [lax.rem(me_x + d, nx) for d in range(1, nx)]
    ys = [me_y] + [lax.rem(me_y + d, ny) for d in range(1, ny)]
    right = {'cp': xs[1] * 2 + core}
    left = {'cp': xs[3] * 2 + core}
    up = {'tp': ys[1]}
    down = {'tp': ys[3]}
    partner = {'cp': me_x * 2 + other}

    barrier = pltpu.get_barrier_semaphore()
    for peer in (right, left, up, down, partner):
        pl.semaphore_signal(barrier, inc=1, device_id=peer, device_id_type=MESH)
    pl.semaphore_wait(barrier, 5)

    def remote(src, dst, ssem, rsem, peer):
        return pltpu.make_async_remote_copy(src_ref=src, dst_ref=dst, send_sem=ssem, recv_sem=rsem, device_id=peer, device_id_type=MESH)

    w_copy = pltpu.make_async_copy(w_hbm, w_ref, w_sem)
    w_copy.start()
    x_copies = []
    for ch in range(num_chunks):
        block = ((ch * nx + me_x) * 2 + core) * ny + me_y
        copy = pltpu.make_async_copy(hid_ref.at[block], xres.at[ch], x_sem.at[ch])
        copy.start()
        x_copies.append(copy)

    rs = [dict() for _ in range(num_chunks)]
    for ch in range(num_chunks):
        for i, xd in enumerate((2, 1, 3, 0)):
            copy = remote(a_ref.at[ch, xs[xd], other], d2d.at[ch, xs[xd]], rs_send.at[ch, i], rs_recv.at[ch, i], partner)
            copy.start()
            rs[ch]['d', xd] = copy

    def stat_of(ref):
        return ref[head_dim:head_dim + 1], ref[head_dim + STAT_ROWS // 2:head_dim + STAT_ROWS // 2 + 1]

    def merged(refs):
        stats = [stat_of(r) for r in refs]
        top = functools.reduce(jnp.maximum, [m for m, _ in stats])
        factors = [jnp.exp2((m - top) * scale) for m, _ in stats]
        total = sum(l * f for (_, l), f in zip(stats, factors))
        mixed = sum(r[:head_dim] * f for r, f in zip(refs, factors))
        return mixed, top, total

    def merge_into(dst, refs):
        mixed, top, total = merged(refs)
        dst[:head_dim] = mixed
        dst[head_dim:] = jnp.where(lax.broadcasted_iota(jnp.int32, (STAT_ROWS, lanes), 0) < STAT_ROWS // 2, top, total)

    def cp_pair(ch):
        for xd in (2, 1, 3, 0):
            rs[ch]['d', xd].wait_recv()
            for kv in range(kv_local):
                dst = d2d.at[ch, xs[xd], kv]
                merge_into(dst, [a_ref.at[ch, xs[xd], core, kv], dst])
            if xd == 2:
                rs[ch]['r1'] = remote(d2d.at[ch, xs[2], 0], step1.at[ch, 0], rs_send.at[ch, 4], rs_recv.at[ch, 4], right)
                rs[ch]['l1'] = remote(d2d.at[ch, xs[2], 1], step1.at[ch, 1], rs_send.at[ch, 5], rs_recv.at[ch, 5], left)
                rs[ch]['r1'].start()
                rs[ch]['l1'].start()

    def cp_step(ch):
        rs[ch]['r1'].wait_recv()
        dst = d2d.at[ch, xs[1], 0]
        merge_into(dst, [dst, step1.at[ch, 0]])
        rs[ch]['r2'] = remote(d2d.at[ch, xs[1]], step2.at[ch, 0], rs_send.at[ch, 6], rs_recv.at[ch, 6], right)
        rs[ch]['r2'].start()
        rs[ch]['l1'].wait_recv()
        dst = d2d.at[ch, xs[3], 1]
        merge_into(dst, [dst, step1.at[ch, 1]])
        rs[ch]['l2'] = remote(d2d.at[ch, xs[3]], step2.at[ch, 1], rs_send.at[ch, 7], rs_recv.at[ch, 7], left)
        rs[ch]['l2'].start()

    def project(ch):
        rs[ch]['r2'].wait_recv()
        rs[ch]['l2'].wait_recv()
        for kv in range(kv_local):
            mixed, _, total = merged([d2d.at[ch, xs[0], kv], step2.at[ch, 0, kv], step2.at[ch, 1, kv]])
            heads = (mixed / total).T.astype(BF16)
            for g in range(group):
                col = (kv * group + g) * head_dim
                heads_ref[:, col:col + head_dim] = heads[g * toks:(g + 1) * toks]
        if ch == 0:
            w_copy.wait()
        tile = width // 10

        @pl.loop(0, 10)
        def _(n):
            at = pl.ds(pl.multiple_of(n * tile, tile), tile)
            product = jnp.dot(heads_ref[...], w_ref[:, at], preferred_element_type=F32).astype(BF16).astype(F32)
            for d in range(ny):
                part[ch, d, :, at] = product[d * rows:(d + 1) * rows]

        low, high = pl.ds(0, half), pl.ds(half, half)
        rs[ch]['u1'] = remote(part.at[ch, ys[2], :, low], tp1.at[ch, 0], rs_send.at[ch, 8], rs_recv.at[ch, 8], up)
        rs[ch]['d1'] = remote(part.at[ch, ys[2], :, high], tp1.at[ch, 1], rs_send.at[ch, 9], rs_recv.at[ch, 9], down)
        rs[ch]['u1'].start()
        rs[ch]['d1'].start()

    def tp_step(ch):
        rs[ch]['u1'].wait_recv()
        part[ch, ys[1], :, :half] += tp1[ch, 0]
        rs[ch]['u2'] = remote(part.at[ch, ys[1]], tp2.at[ch, 0], rs_send.at[ch, 10], rs_recv.at[ch, 10], up)
        rs[ch]['u2'].start()
        rs[ch]['d1'].wait_recv()
        part[ch, ys[3], :, half:] += tp1[ch, 1]
        rs[ch]['d2'] = remote(part.at[ch, ys[3]], tp2.at[ch, 1], rs_send.at[ch, 11], rs_recv.at[ch, 11], down)
        rs[ch]['d2'].start()

    sends = []
    recvs = [dict() for _ in range(num_chunks)]
    q_all = (0, 4)
    q_a, q_b = (0, 2), (2, 2)

    def piece(ch, dx, dy, q):
        return full.at[ch, xs[dx], core, ys[dy], :, pl.ds(q[0] * quarter, q[1] * quarter)]

    used = [0] * num_chunks

    def hop(ch, dx, dy, q, peer, tag):
        n = used[ch]
        used[ch] += 1
        src = piece(ch, dx, dy, q)
        copy = remote(src, src, ag_send.at[ch, n], ag_recv.at[ch, n], peer)
        copy.start()
        sends.append(copy)
        recvs[ch][tag] = copy

    def pair_block(ch, dx, dy):
        n = dx * ny + dy
        src = full.at[ch, xs[dx], core, ys[dy]]
        copy = remote(src, src, pr_send.at[ch, n], pr_recv.at[ch, n], partner)
        copy.start()
        sends.append(copy)
        recvs[ch]['pair', dx, dy] = copy

    def finish(ch):
        x_copies[ch].wait()
        rs[ch]['u2'].wait_recv()
        rs[ch]['d2'].wait_recv()
        summed = part[ch, ys[0]] + tp2[ch, 0] + tp2[ch, 1]
        full[ch, xs[0], core, ys[0]] = (xres[ch].astype(F32) + summed).astype(BF16).astype(F32)
        hop(ch, 0, 0, q_all, right, 'R0')
        hop(ch, 0, 0, q_all, left, 'L0')
        hop(ch, 0, 0, q_all, up, 'U0')
        hop(ch, 0, 0, q_all, down, 'D0')
        pair_block(ch, 0, 0)

    def gather1(ch):
        got = recvs[ch]
        got['R0'].wait_recv()
        hop(ch, 3, 0, q_a, right, 'R1')
        hop(ch, 3, 0, q_a, up, 'U1m')
        hop(ch, 3, 0, q_a, down, 'D1m')
        got['L0'].wait_recv()
        hop(ch, 1, 0, q_b, left, 'L1')
        hop(ch, 1, 0, q_a, up, 'U1p')
        hop(ch, 1, 0, q_a, down, 'D1p')
        got['U0'].wait_recv()
        hop(ch, 0, 3, q_a, up, 'U1')
        hop(ch, 0, 3, q_b, right, 'R1m')
        hop(ch, 0, 3, q_b, left, 'L1m')
        got['D0'].wait_recv()
        hop(ch, 0, 1, q_b, down, 'D1')
        hop(ch, 0, 1, q_b, right, 'R1p')
        hop(ch, 0, 1, q_b, left, 'L1p')
        for dx, dy in ((3, 0), (1, 0), (0, 3), (0, 1)):
            pair_block(ch, dx, dy)

    def gather2(ch):
        got = recvs[ch]
        got['R1'].wait_recv()
        hop(ch, 2, 0, q_a, up, 'U2')
        hop(ch, 2, 0, q_a, down, 'D2')
        got['D1'].wait_recv()
        hop(ch, 0, 2, q_b, right, 'R2')
        hop(ch, 0, 2, q_b, left, 'L2')
        got['L1'].wait_recv()
        got['U1'].wait_recv()
        pair_block(ch, 2, 0)
        pair_block(ch, 0, 2)

    def gather3(ch):
        got = recvs[ch]
        got['U1m'].wait_recv()
        hop(ch, 3, 3, (0, 1), up, 'U3m')
        got['R1m'].wait_recv()
        hop(ch, 3, 3, (2, 1), right, 'R3m')
        pair_block(ch, 3, 3)
        got['D1m'].wait_recv()
        hop(ch, 3, 1, (1, 1), down, 'D3m')
        got['R1p'].wait_recv()
        hop(ch, 3, 1, (2, 1), right, 'R3p')
        pair_block(ch, 3, 1)
        got['U1p'].wait_recv()
        hop(ch, 1, 3, (0, 1), up, 'U3p')
        got['L1m'].wait_recv()
        hop(ch, 1, 3, (3, 1), left, 'L3m')
        pair_block(ch, 1, 3)
        got['D1p'].wait_recv()
        hop(ch, 1, 1, (1, 1), down, 'D3p')
        got['L1p'].wait_recv()
        hop(ch, 1, 1, (3, 1), left, 'L3p')
        pair_block(ch, 1, 1)
        got['U2'].wait_recv()
        hop(ch, 2, 3, (0, 1), up, 'U4')
        got['R2'].wait_recv()
        hop(ch, 3, 2, (2, 1), right, 'R4')
        got['D2'].wait_recv()
        hop(ch, 2, 1, (1, 1), down, 'D4')
        got['L2'].wait_recv()
        hop(ch, 1, 2, (3, 1), left, 'L4')

    def gather4(ch):
        got = recvs[ch]
        got['U3m'].wait_recv()
        got['D3m'].wait_recv()
        pair_block(ch, 3, 2)
        got['U3p'].wait_recv()
        got['D3p'].wait_recv()
        pair_block(ch, 1, 2)
        got['R3m'].wait_recv()
        got['L3m'].wait_recv()
        pair_block(ch, 2, 3)
        got['R3p'].wait_recv()
        got['L3p'].wait_recv()
        pair_block(ch, 2, 1)
        for tag in ('U4', 'R4', 'D4', 'L4'):
            got[tag].wait_recv()
        pair_block(ch, 2, 2)

    outs = []

    def emit(ch):
        for dx in range(nx):
            for dy in range(ny):
                recvs[ch]['pair', dx, dy].wait_recv()

        @pl.loop(0, nx * 2)
        def _(n):
            for d in range(ny):
                stage[ch, n, d * rows:(d + 1) * rows] = full[ch, n // 2, n % 2, d].astype(BF16)

        per = nx * 2
        copy = pltpu.make_async_copy(stage.at[ch], y_hbm.at[pl.ds(ch * per, per)], out_sem.at[ch])
        copy.start()
        outs.append(copy)

    steps = (cp_pair, cp_step, project, tp_step, finish, gather1, gather2, gather3, gather4, emit)
    lag = 1
    for tick in range(len(steps) + lag * (num_chunks - 1)):
        for ch in range(num_chunks):
            if 0 <= tick - lag * ch < len(steps):
                steps[tick - lag * ch](ch)
    for ch in range(num_chunks):
        for copy in rs[ch].values():
            copy.wait_send()
    for copy in sends:
        copy.wait_send()
    for copy in outs:
        copy.wait()


def combine(num_chunks, nx, ny, partial, hidden, w_out, head_dim):
    num_reqs, halves, kv_local, depth, lanes = partial.shape
    total_rows, width = hidden.shape[0] * hidden.shape[1], hidden.shape[2]
    toks = total_rows // (num_chunks * nx * 2)
    rows = toks // ny
    feats = w_out.shape[0]
    a = partial.reshape(num_chunks, nx, 2, kv_local, depth, lanes)
    hid = hidden.reshape(num_chunks * nx * 2 * ny, rows, width)
    scale = head_dim ** -0.5 * math.log2(math.e)
    dma = pltpu.SemaphoreType.DMA
    out = pl.pallas_call(
        functools.partial(combine_kernel, num_chunks, nx, ny, scale),
        in_specs=[pl.BlockSpec(memory_space=pltpu.VMEM), pl.BlockSpec(memory_space=pl.ANY), pl.BlockSpec(memory_space=pl.ANY)],
        out_specs=pl.BlockSpec(memory_space=pl.ANY),
        out_shape=jax.ShapeDtypeStruct((num_chunks * nx * 2, toks, width), BF16),
        scratch_shapes=[
            pltpu.VMEM((feats, width), BF16),
            pltpu.VMEM((num_chunks, rows, width), BF16),
            pltpu.VMEM((num_chunks, nx, kv_local, depth, lanes), F32),
            pltpu.VMEM((num_chunks, 2, depth, lanes), F32),
            pltpu.VMEM((num_chunks, 2, kv_local, depth, lanes), F32),
            pltpu.VMEM((toks, feats), BF16),
            pltpu.VMEM((num_chunks, ny, rows, width), F32),
            pltpu.VMEM((num_chunks, 2, rows, width // 2), F32),
            pltpu.VMEM((num_chunks, 2, rows, width), F32),
            pltpu.VMEM((num_chunks, nx, 2, ny, rows, width), F32),
            pltpu.VMEM((num_chunks, nx * 2, toks, width), BF16),
            dma, dma((num_chunks,)), dma((num_chunks,)),
            dma((num_chunks, 12)), dma((num_chunks, 12)),
            dma((num_chunks, 32)), dma((num_chunks, 32)),
            dma((num_chunks, nx * ny)), dma((num_chunks, nx * ny)),
        ],
        compiler_params=pltpu.CompilerParams(collective_id=0, has_side_effects=True, vmem_limit_bytes=60 * 1024 * 1024),
        name="combine",
    )(a, hid, w_out)
    return out.reshape(hidden.shape)


def solution(mesh):
    cp_size, tp_size = mesh.shape['cp'], mesh.shape['tp']
    cache_spec = P('dp', None, 'cp', 'tp')
    row_spec = P('dp')

    def local_step(hidden, attn_gain, w_query, w_key, w_value, w_out, cache_k, cache_v, ctx_len, positions, tree_mask):
        num_reqs, tree_len, width = hidden.shape
        head_dim = cache_k.shape[5]
        halves = max(1, NUM_CHUNKS * cp_size // num_reqs)
        cos_tab, sin_tab = rope_tables(positions, head_dim)
        q, kn, vn = project_qkv(hidden.reshape(num_reqs * tree_len, width), attn_gain[None, :], cos_tab, sin_tab, w_query, w_key, w_value)
        cp_rank = lax.axis_index('cp').astype(jnp.int32).reshape(1)
        partial, new_k, new_v = attend(cp_size, halves, ctx_len, cp_rank, q, kn, vn, tree_mask, cache_k, cache_v)
        out = combine(NUM_CHUNKS, cp_size // 2, tp_size, partial, hidden, w_out, head_dim)
        return out, new_k, new_v

    return jax.shard_map(local_step, mesh=mesh, in_specs=(row_spec, P(), P(None, 'tp'), P(None, 'tp'), P(None, 'tp'), P('tp', None), cache_spec, cache_spec, row_spec, row_spec, row_spec), out_specs=(row_spec, cache_spec, cache_spec), check_vma=False)
```

time: 656 us -> 184 us (0.28); the launches traced: 647 us -> 183 us
  local copies, waits for them, and re-layouts: 288 us -> 10.4 us
  Pallas kernels: 0 us -> 168 us
  waiting for transfers between devices: 141 us -> 0 us
  matrix products: 94.6 us -> 0 us
  other arithmetic: 57.3 us -> 3.93 us
  blocking collectives: 50.4 us -> 0 us
  between operations: 14.8 us -> 0.65 us
    unnamed x35 -> x1, local copies, waits for them, and re-layouts: 261 us -> 9.05 us
    pallas_call x0 -> x3, Pallas kernels: none -> 168 us  [the longest x1 111 us: combine(): pl.pallas_call(functools.partial(combine_kernel, num_chunks, nx, ny, scal...]
    psum x2 -> x0, waiting for transfers between devices: 141 us -> none  [the longest x1 97.5 us: local_step(): proj_sum = lax.psum(proj_part.astype(jnp.float32), 'tp')]
    dot_general x8 -> x0, matrix products: 94.6 us -> none  [the longest x1 19.3 us: local_step(): jnp.einsum('rtkgji,rjkid->rtkgd', prob_cache.astype(jnp.bfloat16), values...]
    psum x1 -> x0, blocking collectives: 25.8 us -> none  [local_step(): glob_sum = lax.psum(row_sum * factor, 'cp')]
    reduce_sum x3 -> x0, other arithmetic: 25.1 us -> none  [the longest x2 19 us: local_step(): row_sum = prob_cache.sum(axis=(4, 5)) + prob_tree.sum(axis=-1)]
    pmax x1 -> x0, blocking collectives: 24.7 us -> none  [local_step(): glob_max = lax.pmax(row_max, 'cp')]
    convert_element_type x5 -> x1, other arithmetic: 25.2 us -> 0.7 us  [rope_tables(): angle = positions.astype(F32).reshape(-1)[:, None] * inv_freq]
  transfers between devices with their start and end apart: 2 -> 0, of which waited for: 2 -> 0; matrix products, arithmetic and copies ran while one was open for 41% -> 0% of each run, Pallas kernels for 0% -> 0%
where the time goes in v1:
time: 184 us; the launch traced here: 183 us
  Pallas kernels  168 us (91%)
  local copies, waits for them, and re-layouts  10.4 us (6%)
  other arithmetic  3.93 us (2%)
    pallas_call x1, Pallas kernels, combine(): pl.pallas_call(functools.partial(combine_kernel, num_chunks, nx, ny, scal...  111 us
    pallas_call x1, Pallas kernels, attend(): pl.pallas_call(functools.partial(attn_kernel, cp_size, halves), grid_spec...  29.8 us
    pallas_call x1, Pallas kernels, project_qkv(): pl.pallas_call(qkv_kernel, grid=(rows // tile,), in_specs=[row_block(widt...  27.7 us
    unnamed x1, local copies, waits for them, and re-layouts  9.05 us

profile of v1, /device:TPU:97, one launch (start us, length us, event | category | flops | bytes accessed | tf_op | source)
XLA Modules:
  0.0 183.3 jit_solution(3705901365665467798)
XLA Ops:
  0.7 0.7 convert_element_type.3
  1.4 0.1 mul.31
  1.4 1.3 broadcast_in_dim.4.gain_ref
  2.8 1.9 %fusion = (f32[1024,64]{1,0:T(8,128)S(1)}, f32[1024,64]{1,0:T(8,128)S(1)}, f32[1024,64]{1,0:T(8,128)S(1)}) fusion(f32[64]{0:T(128)S(1)} %compare_select_fusion.1, f32[1024]{0:T(1024)S(1)} %mul.31), kind=kLoop, calls=%fused_computation.4 | loop fusion | flops 131072 | bytes 790784 | tf_op jit(solution)/shard_map/neg | solution.py:30
  4.7 1.3 pad_maximum_fusion
  6.0 27.7 %qkv.1 = (bf16[1024,1024]{1,0:T(8,128)(2,1)}, bf16[1024,256]{1,0:T(8,128)(2,1)}, bf16[1024,256]{1,0:T(8,128)(2,1)}) custom-call(bf16[1024,5120]{1,0:T(8,128)(2,1)} %bitcast.4, bf16[1,5120]{1,0:T(2,128)(2,1)} %broadcast_in_dim.4.gain_ref, f32[1024,128]{1,0:T(8,128)} %get-tuple-element.18.cos_ref, f32[1024,128]{1,0:T(8,128)} %get-tuple-element.19.sin_ref, ...), custom_call_target="tpu_custom_call" | custom-call | tf_op jit(solution)/shard_map/qkv/pallas_call | solution.py:55
  33.6 29.8 %attn.1 = (f32[16,1,2,136,256]{4,3,2,1,0:T(8,128)}, bf16[16,4,1,2,256,128]{5,4,3,2,1,0:T(8,128)(2,1)}, bf16[16,4,1,2,256,128]{5,4,3,2,1,0:T(8,128)(2,1)}) custom-call(s32[16]{0:T(128)} %ctx_ref.1, s32[1]{0:T(128)} %bitcast.cp_ref, bf16[1024,1024]{1,0:T(8,128)(2,1)} %get-tuple-element.9.q_ref, bf16[1024,256]{1,0:T(8,128)(2,1)} %get-tuple-element.10.kn_ref, ...), custom_call_target="tpu_custom_call" | custom-call | tf_op jit(solution)/shard_map/attn/pallas_call | solution.py:133
  63.5 110.8 %combine.1 = bf16[16,64,5120]{2,1,0:T(8,128)(2,1)} custom-call(f32[2,4,2,2,136,256]{5,4,3,2,1,0:T(8,128)} %bitcast.6, bf16[64,16,5120]{2,1,0:T(8,128)(2,1)} %bitcast.5, bf16[1024,5120]{1,0:T(8,128)(2,1)} %w_hbm.1), custom_call_target="tpu_custom_call" | custom-call | tf_op jit(solution)/shard_map/combine/pallas_call | solution.py:432
  174.2 9.0 %copy.15 = bf16[16,64,5120]{2,1,0:T(8,128)(2,1)} copy(bf16[16,64,5120]{2,1,0:T(8,128)(2,1)} %combine.1) | data formatting | bytes 20971520
  (1 shorter events, 0.0 us)
